TPU v7x, 32 devices: a whole 2x2x4 slice. The times are simulated.
32 devices in a mesh: rep: 2 (over x), tp: 8 (over z, y), sub: 2 (over core).
Axes of the slice: x: 2, y: 2, z: 4, core: 2. Of those that a mesh axis runs over, the one named last changes fastest.
Arguments:
- attention: bfloat16 [1024, 8192], P('rep', ('tp', 'sub')), parts along dimension 0, may hold values from -6 to 6
- out_weight: bfloat16 [8192, 8192], P(('tp', 'sub')), may hold values from -0.09375 to 0.09375
- residual: bfloat16 [1024, 8192], P('rep', ('tp', 'sub')), parts along dimension 0, may hold values from -6 to 6
- norm_gain: bfloat16 [8192], P(('tp', 'sub')), may hold values from 0.25 to 1.75
Outputs:
- quantized: bfloat16 [1024, 8192], P('rep'), parts along dimension 0
- scales: bfloat16 [1024, 64], P('rep'), parts along dimension 0
- new_residual: bfloat16 [1024, 8192], P('rep', ('tp', 'sub')), parts along dimension 0
There are 2 independent parts, one for each index of `rep`. A program takes and returns all parts, laid end to end along the dimension named above; an argument that names none is the same for every part. Nothing has to cross between parts.
All inputs are finite; a program needn't handle non-finite values.
Results may differ from a plain program's by a relative error of at most 0.0048.
Values may be sent and summed in bfloat16 or wider, within the bound.
No kernel may reach another device: no remote copies, remote signals or barrier semaphores. Data moves between devices by JAX's collectives and lax.ppermute only.
A program may use at most 128 MiB of HBM per device.

v0:
```python
import jax
import jax.numpy as jnp
from jax import lax
from jax.sharding import PartitionSpec as P

BLOCK = 128


epsilon = 0.1
floor_scale = 0.5


def per_device(attention, out_weight, residual, norm_gain):
    width_all = out_weight.shape[1]
    summed = lax.psum_scatter(
        lax.dot_general(
            out_weight, attention, (((0,), (1,)), ((), ())), preferred_element_type=jnp.float32
        ),
        ("tp", "sub"),
        scatter_dimension=0,
        tiled=True,
    )
    hidden = residual.astype(jnp.float32) + summed.T
    new_residual = hidden.astype(jnp.bfloat16)
    squares = lax.psum(jnp.sum(hidden * hidden, axis=1), ("tp", "sub"))
    mean_square = squares / width_all
    normed = hidden * lax.rsqrt(mean_square + epsilon)[:, None] * norm_gain.astype(jnp.float32)
    blocks = normed.reshape(hidden.shape[0], hidden.shape[1] // BLOCK, BLOCK)
    largest = jnp.max(jnp.abs(blocks), axis=2)
    scales = jnp.maximum(largest, floor_scale).astype(jnp.bfloat16)
    quantized = (
        (blocks / scales.astype(jnp.float32)[:, :, None]).reshape(hidden.shape).astype(jnp.bfloat16)
    )
    full_quant, full_scales = (
        lax.all_gather(quantized, ("tp", "sub"), axis=1, tiled=True),
        lax.all_gather(scales, ("tp", "sub"), axis=1, tiled=True),
    )
    return (full_quant, full_scales, new_residual)


def solution(mesh):
    in_specs = (
        P("rep", ("tp", "sub")),
        P(("tp", "sub"), None),
        P("rep", ("tp", "sub")),
        P(("tp", "sub")),
    )
    out_specs = (P("rep", None), P("rep", None), P("rep", ("tp", "sub")))
    return jax.shard_map(
        per_device, mesh=mesh, in_specs=in_specs, out_specs=out_specs, check_vma=False
    )
```

profile of v0, /device:TPU:0, one launch (start us, length us, event | category | flops | bytes accessed | tf_op | source)
XLA Modules:
  0.0 327.3 jit_solution(3654953643072817745)
XLA Ops:
  7.2 0.0 copy-start
  7.2 0.0 reduce-scatter.2.cloned.1.call-start
  7.2 1.0 copy-done
  8.2 11.7 %fusion.5 = f32[8192,512]{1,0:T(8,128)} fusion(bf16[512,8192]{1,0:T(8,128)(2,1)} %param.5, bf16[512,512]{1,0:T(8,128)(2,1)S(1)} %copy-done), kind=kOutput, calls=%fused_computation.12 | convolution fusion | flops 4294967296 | bytes 25690112 | tf_op jit(solution)/shard_map/dot_general | solution.py:16
  19.9 0.0 copy-start.1
  19.9 0.0 copy-start.2
  19.9 0.0 reduce-scatter.2.cloned.1.call-update
  19.9 0.0 all-gather.3.cloned.1.call-start
  20.0 1.0 copy-done.1
  20.9 0.2 copy.10
  21.2 0.0 copy-done.2
  21.2 179.0 %reduce-scatter.2.cloned.1.call-done = f32[512,512]{1,0:T(8,128)} async-done(((f32[8192,512]{1,0:T(8,128)}), f32[512,512]{1,0:T(8,128)}) %reduce-scatter.2.cloned.1.call-update) | async-done | bytes 1048592 | tf_op jit(solution)/shard_map/reduce_scatter | solution.py:15
  200.1 1.4 multiply_reduce_fusion
  201.5 31.5 %psum.7 = f32[512]{0:T(512)S(1)} all-reduce(f32[512]{0:T(512)S(1)} %multiply_reduce_fusion), channel_id=1, replica_groups=mesh['rep'=2,'tp'=8,'sub'=2] {'tp','sub'}, use_global_device_ids=true, to_apply=%region_2.0 | all-reduce | flops 512 | bytes 4096 | tf_op jit(solution)/shard_map/psum | solution.py:25
  233.1 1.4 bitcast_reduce_fusion
  234.5 2.2 fusion.2
  236.7 0.0 all-gather.3.cloned.1.call-update
  236.8 1.0 copy.12
  237.8 17.8 %all-gather = bf16[16,4,512]{2,1,0:T(4,128)(2,1)S(1)} all-gather(bf16[1,4,512]{2,1,0:T(4,128)(2,1)S(1)} %get-tuple-element.11), channel_id=1, replica_groups=mesh['rep'=2,'tp'=8,'sub'=2] {'tp','sub'}, dimensions={0}, use_global_device_ids=true | all-gather | bytes 69632 | tf_op jit(solution)/shard_map/all_gather | solution.py:36
  255.6 0.6 reshape.18
  256.2 52.3 %all-gather.3.cloned.1.call-done = bf16[512,8192]{0,1:T(8,128)(2,1)} async-done(((bf16[512,512]{0,1:T(8,128)(2,1)}), bf16[512,8192]{0,1:T(8,128)(2,1)}) %all-gather.3.cloned.1.call-update) | async-done | bytes 8388624 | tf_op jit(solution)/shard_map/all_gather | solution.py:35
  308.6 11.9 %copy.11 = bf16[512,8192]{1,0:T(8,128)(2,1)} copy(bf16[512,8192]{0,1:T(8,128)(2,1)} %all-gather.3.cloned.1.call-done) | data formatting | bytes 16777216
  (3 shorter events, 0.0 us)
Async XLA Ops:
  7.2 1.0 copy-start
  7.2 193.0 %reduce-scatter.2.cloned.1.call-start = ((), (), s32[]{:S(2)}) async-start(), calls=%async_computation.1 | async-start | bytes 17825792 | tf_op jit(solution)/shard_map/reduce_scatter | solution.py:15
  19.9 1.0 copy-start.1
  19.9 1.3 copy-start.2
  19.9 288.6 %all-gather.3.cloned.1.call-start = ((), (), s32[]{:S(2)}) async-start(), calls=%async_computation.2 | async-start | bytes 8912896 | tf_op jit(solution)/shard_map/all_gather | solution.py:35
Sparse Core Ops, SparseCore 0:
  20.0 180.0 reduce-scatter.1
  236.9 71.6 all-gather.2
where the time goes:
time: 328 us; the launch traced here: 327 us
  waiting for transfers between devices  231 us (70%)
  blocking collectives  49.3 us (15%)
  local copies, waits for them, and re-layouts  15.7 us (5%)
  between operations  14.1 us (4%)
  matrix products  11.7 us (4%)
  other arithmetic  5.1 us (2%)
    reduce_scatter x1, waiting for transfers between devices, per_device(): lax.psum_scatter(lax.dot_general(out_weight, attention, (((0,), (1,)), ((...  179 us
    all_gather x1, waiting for transfers between devices, per_device(): lax.all_gather(quantized, ('tp', 'sub'), axis=1, tiled=True)  52.3 us
    psum x1, blocking collectives, per_device(): squares = lax.psum(jnp.sum(hidden * hidden, axis=1), ('tp', 'sub'))  31.5 us
    all_gather x1, blocking collectives, per_device(): lax.all_gather(scales, ('tp', 'sub'), axis=1, tiled=True)  17.8 us
    unnamed x10, local copies, waits for them, and re-layouts  15.7 us
    dot_general x1, matrix products, per_device(): lax.dot_general(out_weight, attention, (((0,), (1,)), ((), ())), preferre...  11.7 us
  transfers between devices with their start and end apart: 2, of which 2 were waited for; matrix products, arithmetic and copies ran while one was open for 1% of the time, Pallas kernels for 0%

commit v1 on v0

v1 whole, which is shorter than its diff:
```python
import functools

import jax
import jax.numpy as jnp
from jax import lax
from jax.experimental import pallas as pl
from jax.experimental.pallas import tpu as pltpu
from jax.sharding import PartitionSpec as P

BLOCK = 128
LANES = 128
TAIL = 8
SHORT_RING = 8

epsilon = 0.1
floor_scale = 0.5


def cost(flops, moved):
    return pl.CostEstimate(flops=int(flops), bytes_accessed=int(moved), transcendentals=0)


def ring_order(mesh):
    natural = list(range(mesh.shape["tp"]))
    snake = natural[0::2] + natural[1::2][::-1]
    place = [getattr(d, "coords", None) for d in mesh.devices[0, :, 0]]
    if None in place:
        return natural

    def length(order):
        pairs = zip(order, order[1:] + order[:1])
        return sum(sum(abs(i - j) for i, j in zip(place[a], place[b])) for a, b in pairs)

    return min((natural, snake), key=length)


def pick_kernel(width, spot, weight, out, sem):
    copies = []
    for k in range(out.shape[0]):
        column = pl.multiple_of(spot[k] * width, width)
        copies.append(pltpu.make_async_copy(weight.at[:, pl.ds(column, width)], out.at[k], sem.at[k]))
    for copy in copies:
        copy.start()
    for copy in copies:
        copy.wait()


def partial_kernel(spot, own, far, weight_own, weight_far, top, bottom):
    half = top.shape[1]
    for k, out in enumerate((top, bottom)):
        part = pl.ds(k * half, half)
        total = jnp.dot(own[part, :], weight_own[...], preferred_element_type=jnp.float32)
        total = total + jnp.dot(far[part, :], weight_far[0], preferred_element_type=jnp.float32)
        out[0] = total.astype(out.dtype)


def hidden_kernel(own, residual, first, second, hidden, rounded, squares):
    rows, width = hidden.shape
    for row in range(0, rows, LANES):
        part = pl.ds(row, LANES)
        value = own[0, part, :] + residual[part, :].astype(jnp.float32)
        value = value + first[part, :].astype(jnp.float32) + second[part, :].astype(jnp.float32)
        hidden[part, :] = value
        rounded[part, :] = value.astype(jnp.bfloat16)
        square = value * value
        total = square[:, :LANES]
        for column in range(LANES, width, LANES):
            total = total + square[:, column : column + LANES]
        squares[0:1, part] = jnp.sum(total.T, axis=0, keepdims=True)


def quantize_kernel(width_all, squares, hidden, gain, out):
    rows, width = hidden.shape
    per = width // BLOCK
    lane = lax.broadcasted_iota(jnp.int32, (LANES, LANES), 1)
    for chunk in range(rows // LANES):
        part = pl.ds(chunk * LANES, LANES)
        inverse = lax.rsqrt(squares[0:1, part] / width_all + epsilon)
        inverse = jnp.broadcast_to(inverse, (LANES, LANES)).T
        gathered = jnp.zeros((LANES, LANES), jnp.float32)
        for b in range(per):
            columns = pl.ds(b * BLOCK, BLOCK)
            normed = hidden[part, columns] * inverse * gain[0:1, columns].astype(jnp.float32)
            largest = jnp.max(jnp.abs(normed), axis=1, keepdims=True)
            scale = jnp.maximum(largest, floor_scale).astype(jnp.bfloat16).astype(jnp.float32)
            out[part, columns] = (normed / scale).astype(jnp.bfloat16)
            gathered = jnp.where(lane == b, scale, gathered)
        line, column = divmod(chunk, width // LANES)
        turned = gathered.T.astype(jnp.bfloat16)
        out[pl.ds(rows + line * per, per), pl.ds(column * LANES, LANES)] = turned[:per]


def place_kernel(starts, fresh, spot, *refs):
    blocks = refs[: len(starts)]
    full, tails, sem = refs[-3:]
    copies = []
    for k, (start, block) in enumerate(zip(starts, blocks)):
        rows, width = block.shape[0] - TAIL, block.shape[1]
        column = pl.multiple_of(spot[k] * width, width)
        line = pl.multiple_of(spot[k] * TAIL, TAIL)
        copies.append(
            pltpu.make_async_copy(
                block.at[pl.ds(0, rows)],
                full.at[pl.ds(start * rows, rows), pl.ds(column, width)],
                sem.at[0, k],
            )
        )
        copies.append(
            pltpu.make_async_copy(block.at[pl.ds(rows, TAIL)], tails.at[start, pl.ds(line, TAIL)], sem.at[1, k])
        )
    for copy in copies:
        copy.start()
    for copy in copies:
        copy.wait()


def make_per_device(mesh):
    order = ring_order(mesh)
    n, m = mesh.shape["tp"], mesh.shape["sub"]
    link_type = jnp.bfloat16 if n <= SHORT_RING else jnp.float32
    where = [order.index(t) for t in range(n)]
    far = n // 2

    def forward(x, hops):
        return lax.ppermute(x, "tp", [(order[i], order[(i + hops) % n]) for i in range(n)])

    def across(x):
        return lax.ppermute(x, "sub", [(i, (i + 1) % m) for i in range(m)])

    def everywhere(x):
        x = x + across(x)
        bit = 1
        while bit < n:
            x = x + lax.ppermute(x, "tp", [(t, t ^ bit) for t in range(n)])
            bit *= 2
        return x

    def per_device(attention, out_weight, residual, norm_gain):
        rows, width = residual.shape
        depth, width_all = out_weight.shape
        half = rows // 2
        per = width // BLOCK
        tp, core = lax.axis_index("tp"), lax.axis_index("sub")
        other = (core + 1) % m
        position = jnp.array(where, jnp.int32)[tp]
        owners = jnp.array(order, jnp.int32)

        def spots(hops, which):
            return owners[(position + jnp.array(hops, jnp.int32)) % n] * m + which

        def pick(hops):
            count = len(hops)
            return pl.pallas_call(
                functools.partial(pick_kernel, width),
                in_specs=[pl.BlockSpec(memory_space=pltpu.SMEM), pl.BlockSpec(memory_space=pl.ANY)],
                out_specs=pl.BlockSpec(memory_space=pltpu.VMEM),
                out_shape=jax.ShapeDtypeStruct((count, depth, width), jnp.bfloat16),
                scratch_shapes=[pltpu.SemaphoreType.DMA((count,))],
                compiler_params=pltpu.CompilerParams(vmem_limit_bytes=8 << 20),
                cost_estimate=cost(count * 1e8, count * depth * width * 4),
            )(spots(hops, other), out_weight)

        attention_far = across(attention)

        def partials(hops, out_type):
            count = len(hops)
            weight_far = across(pick(hops))
            return pl.pallas_call(
                partial_kernel,
                grid_spec=pltpu.PrefetchScalarGridSpec(
                    num_scalar_prefetch=1,
                    grid=(count,),
                    in_specs=[
                        pl.BlockSpec((rows, depth), lambda i, spot: (0, 0)),
                        pl.BlockSpec((rows, depth), lambda i, spot: (0, 0)),
                        pl.BlockSpec((depth, width), lambda i, spot: (0, spot[i])),
                        pl.BlockSpec((1, depth, width), lambda i, spot: (i, 0, 0)),
                    ],
                    out_specs=[pl.BlockSpec((1, half, width), lambda i, spot: (i, 0, 0))] * 2,
                ),
                out_shape=[jax.ShapeDtypeStruct((count, half, width), out_type)] * 2,
                compiler_params=pltpu.CompilerParams(vmem_limit_bytes=16 << 20),
                cost_estimate=cost(4 * count * rows * depth * width, 4 * count * depth * width),
            )(spots(hops, core), attention, attention_far, out_weight, weight_far)

        groups = [[far], [far - 1, 1 - far], [s * k for k in range(far - 2, 0, -1) for s in (1, -1)] + [0]]
        groups = [[k for k in group if -far < k <= far] for group in groups]
        terms = {}
        for g, group in enumerate(groups):
            halves = partials(group, jnp.float32 if g else link_type)
            for i, k in enumerate(group):
                terms[k % n] = [h[i] for h in halves]
            own = halves

        arrived = {}
        for k in range(far, 0, -1):
            for part, sign in ((0, 1), (1, -1)):
                for direction in (sign, -sign):
                    if k == far and direction != sign:
                        continue
                    term = terms[direction * k % n][part]
                    if (part, direction) in arrived:
                        term = term + arrived[part, direction].astype(jnp.float32)
                    arrived[part, direction] = forward(term.astype(link_type), direction)

        hiddens, residuals, squares = [], [], []
        for part in range(2):
            hidden, rounded, square = pl.pallas_call(
                hidden_kernel,
                grid=(1,),
                in_specs=[
                    pl.BlockSpec((1, half, width), lambda i: (len(groups[-1]) - 1, 0, 0)),
                    pl.BlockSpec((half, width), lambda i, part=part: (part, 0)),
                    pl.BlockSpec((half, width), lambda i: (0, 0)),
                    pl.BlockSpec((half, width), lambda i: (0, 0)),
                ],
                out_specs=[
                    pl.BlockSpec((half, width), lambda i: (0, 0)),
                    pl.BlockSpec((half, width), lambda i: (0, 0)),
                    pl.BlockSpec((1, half), lambda i: (0, 0)),
                ],
                out_shape=[
                    jax.ShapeDtypeStruct((half, width), jnp.float32),
                    jax.ShapeDtypeStruct((half, width), jnp.bfloat16),
                    jax.ShapeDtypeStruct((1, half), jnp.float32),
                ],
                compiler_params=pltpu.CompilerParams(vmem_limit_bytes=16 << 20),
                cost_estimate=cost(1e8, 8 * half * width),
            )(own[part], residual, arrived[part, 1], arrived[part, -1])
            hiddens.append(hidden)
            residuals.append(rounded)
            squares.append(square)
        square = everywhere(jnp.concatenate(squares, axis=0))

        full = tails = None

        def place(pieces, full, tails):
            starts = [part for part, _, _ in pieces]
            blocks = [block for _, _, block in pieces]
            spot = jnp.concatenate([spots([hop], which) for _, (hop, which), _ in pieces])
            shapes = [
                jax.ShapeDtypeStruct((rows, width_all), jnp.bfloat16),
                jax.ShapeDtypeStruct((2, n * m * TAIL, width), jnp.bfloat16),
            ]
            more = [] if full is None else [full, tails]
            return pl.pallas_call(
                functools.partial(place_kernel, starts, not more),
                in_specs=[pl.BlockSpec(memory_space=pltpu.SMEM)]
                + [pl.BlockSpec(memory_space=pltpu.VMEM)] * len(blocks)
                + [pl.BlockSpec(memory_space=pl.ANY)] * len(more),
                out_specs=[pl.BlockSpec(memory_space=pl.ANY)] * 2,
                out_shape=shapes,
                scratch_shapes=[pltpu.SemaphoreType.DMA((2, len(blocks)))],
                input_output_aliases={1 + len(blocks): 0, 2 + len(blocks): 1} if more else {},
                compiler_params=pltpu.CompilerParams(vmem_limit_bytes=16 << 20),
                cost_estimate=cost(1e8, 4 * len(blocks) * half * width),
            )(spot, *blocks, *more)

        held = {}
        for part in range(2):
            held[part, 1] = held[part, -1] = pl.pallas_call(
                functools.partial(quantize_kernel, width_all),
                grid=(1,),
                in_specs=[
                    pl.BlockSpec((1, half), lambda i: (0, 0)),
                    pl.BlockSpec((half, width), lambda i: (0, 0)),
                    pl.BlockSpec((1, width), lambda i: (0, 0)),
                ],
                out_specs=pl.BlockSpec((half + TAIL, width), lambda i: (0, 0)),
                out_shape=jax.ShapeDtypeStruct((half + TAIL, width), jnp.bfloat16),
                compiler_params=pltpu.CompilerParams(vmem_limit_bytes=16 << 20),
                cost_estimate=cost(1e8, 8 * half * width),
            )(square[part : part + 1], hiddens[part], norm_gain[None])
        pieces = []
        for part in range(2):
            block = held[part, 1]
            pieces += [(part, (0, core), block), (part, (0, other), across(block))]
        waiting = pieces
        for k in range(1, far + 1):
            pieces = []
            for part, sign in ((0, 1), (1, -1)):
                for direction in (sign, -sign):
                    if k == far and direction != sign:
                        continue
                    block = held[part, direction] = forward(held[part, direction], direction)
                    hop = -direction * k
                    pieces += [(part, (hop, core), block), (part, (hop, other), across(block))]
            full, tails = place(waiting, full, tails)
            waiting = pieces
        full, tails = place(waiting, full, tails)
        fold = max(1, half // width)
        scales = tails.reshape(2, n * m, TAIL, width)[:, :, : per * fold, : min(half, width)]
        scales = scales.reshape(2, n * m, fold, per, half // fold).transpose(1, 3, 0, 2, 4)
        return (full, scales.reshape(n * m * per, rows).T, jnp.concatenate(residuals, axis=0))

    return per_device


def solution(mesh):
    in_specs = (
        P("rep", ("tp", "sub")),
        P(("tp", "sub"), None),
        P("rep", ("tp", "sub")),
        P(("tp", "sub")),
    )
    out_specs = (P("rep", None), P("rep", None), P("rep", ("tp", "sub")))
    return jax.shard_map(
        make_per_device(mesh), mesh=mesh, in_specs=in_specs, out_specs=out_specs, check_vma=False
    )
```

time: 328 us -> 168 us (0.51)
  waiting for transfers between devices: 231 us -> 65.3 us
  blocking collectives: 49.3 us -> 0 us
  starting transfers between devices: 0.08 us -> 38.4 us
  Pallas kernels: 0 us -> 21.7 us
  matrix products: 11.7 us -> 0 us
  local copies, waits for them, and re-layouts: 15.7 us -> 22.7 us
    reduce_scatter x1 -> x0, waiting for transfers between devices: 179 us -> none  [per_device(): lax.psum_scatter(lax.dot_general(out_weight, attention, (((0,), (1,)), ((...]
    ppermute x0 -> x52, waiting for transfers between devices: none -> 65.3 us  [the longest x28 55.5 us: forward(): lax.ppermute(x, 'tp', [(order[i], order[(i + hops) % n]) for i in range(n)])]
    all_gather x1 -> x0, waiting for transfers between devices: 52.3 us -> none  [per_device(): lax.all_gather(quantized, ('tp', 'sub'), axis=1, tiled=True)]
    ppermute x0 -> x52, starting transfers between devices: none -> 38.4 us  [the longest x28 30.7 us: forward(): lax.ppermute(x, 'tp', [(order[i], order[(i + hops) % n]) for i in range(n)])]
    psum x1 -> x0, blocking collectives: 31.5 us -> none  [per_device(): squares = lax.psum(jnp.sum(hidden * hidden, axis=1), ('tp', 'sub'))]
    pallas_call x0 -> x15, Pallas kernels: none -> 21.7 us  [the longest x5 10.1 us: place(): pl.pallas_call(functools.partial(place_kernel, starts, not more), in_spec...]
    all_gather x1 -> x0, blocking collectives: 17.8 us -> none  [per_device(): lax.all_gather(scales, ('tp', 'sub'), axis=1, tiled=True)]
    dot_general x1 -> x0, matrix products: 11.7 us -> none  [per_device(): lax.dot_general(out_weight, attention, (((0,), (1,)), ((), ())), preferre...]
  transfers between devices with their start and end apart: 2 -> 52, of which waited for: 2 -> 23; matrix products, arithmetic and copies ran while one was open for 1% -> 3% of each run, Pallas kernels for 0% -> 10%
where the time goes in v1:
time: 168 us
  waiting for transfers between devices  65.3 us (39%)
  starting transfers between devices  38.4 us (23%)
  local copies, waits for them, and re-layouts  22.7 us (14%)
  Pallas kernels  21.7 us (13%)
  between operations  14.7 us (9%)
  other arithmetic  4.78 us (3%)
    ppermute x28, waiting for transfers between devices, forward(): lax.ppermute(x, 'tp', [(order[i], order[(i + hops) % n]) for i in range(n)])  55.5 us
    ppermute x28, starting transfers between devices, forward(): lax.ppermute(x, 'tp', [(order[i], order[(i + hops) % n]) for i in range(n)])  30.7 us
    unnamed x61, local copies, waits for them, and re-layouts  18.4 us
    pallas_call x5, Pallas kernels, place(): pl.pallas_call(functools.partial(place_kernel, starts, not more), in_spec...  10.1 us
    pallas_call x3, Pallas kernels, partials(): pl.pallas_call(partial_kernel, grid_spec=pltpu.PrefetchScalarGridSpec(num...  7.13 us
    ppermute x3, waiting for transfers between devices, everywhere(): x = x + lax.ppermute(x, 'tp', [(t, t ^ bit) for t in range(n)])  7 us
    ppermute x3, starting transfers between devices, everywhere(): x = x + lax.ppermute(x, 'tp', [(t, t ^ bit) for t in range(n)])  4.77 us
  transfers between devices with their start and end apart: 52, of which 23 were waited for; matrix products, arithmetic and copies ran while one was open for 3% of the time, Pallas kernels for 10%

profile of v1, /device:TPU:0, one launch (start us, length us, event | category | flops | bytes accessed | tf_op | source)
XLA Modules:
  0.0 167.5 jit_solution(4633035999538708098)
XLA Ops:
  0.6 1.2 dynamic_slice.3
  1.9 1.3 compare_select_fusion.1
  3.2 1.3 gather_fusion
  4.5 3.4 %copy-done = bf16[512,8192]{1,0:T(8,128)(2,1)S(1)} copy-done((bf16[512,8192]{1,0:T(8,128)(2,1)S(1)}, bf16[512,8192]{1,0:T(8,128)(2,1)}, u32[]{:S(2)}) %copy-start) | copy-done | bytes 8388632
  7.9 2.5 %shard_map.427 = bf16[5,512,512]{2,1,0:T(8,128)(2,1)} custom-call(s32[5]{0:T(128)S(1)} %get-tuple-element.244.spot, bf16[512,8192]{1,0:T(8,128)(2,1)S(1)} %copy-done), custom_call_target="tpu_custom_call" | custom-call | flops 500000000 | bytes 5242880 | tf_op jit(solution)/shard_map/pallas_call | solution.py:153
  12.3 3.4 %copy-done.1 = bf16[512,8192]{1,0:T(8,128)(2,1)S(1)} copy-done((bf16[512,8192]{1,0:T(8,128)(2,1)S(1)}, bf16[512,8192]{1,0:T(8,128)(2,1)}, u32[]{:S(2)}) %copy-start.1) | copy-done | bytes 8388632
  26.6 1.6 collective-permute-done.3.weight_far
  28.9 2.9 %collective-permute-start.4 = (bf16[256,512]{1,0:T(8,128)(2,1)S(1)}, bf16[256,512]{1,0:T(8,128)(2,1)S(1)}, u32[]{:S(2)}, u32[]{:S(2)}) collective-permute-start(bf16[256,512]{1,0:T(8,128)(2,1)S(1)} %bitcast.71), channel_id=1, source_target_pairs={{0,4},{4,8},{8,12},{12,14},{14,10},{10,6},{6,2},{2,0},{1,5},{5,9},... | collective-permute-start | bytes 786440 | tf_op jit(solution)/shard_map/ppermute | solution.py:125
  31.8 2.1 %shard_map.430 = (f32[2,256,512]{2,1,0:T(8,128)S(1)}, f32[2,256,512]{2,1,0:T(8,128)S(1)}) custom-call(s32[2]{0:T(128)S(1)} %get-tuple-element.243.spot, bf16[512,512]{1,0:T(8,128)(2,1)S(1)} %copy-done.3, bf16[512,512]{1,0:T(8,128)(2,1)S(1)} %collective-permute-done.far, bf16[512,8192]{1,0:T(8,128)(2,1)S(1)} %copy-done.2, ...), custom_call_target="tpu_custom_call" | custom-call | flops 1073741824 | bytes 2097152 | tf_op jit(solution)/shard_map/pallas_call | solution.py:168
  34.0 2.0 %collective-permute-start.8 = (bf16[256,512]{1,0:T(8,128)(2,1)S(1)}, bf16[256,512]{1,0:T(8,128)(2,1)S(1)}, u32[]{:S(2)}, u32[]{:S(2)}) collective-permute-start(bf16[256,512]{1,0:T(8,128)(2,1)S(1)} %fusion.10), channel_id=1, source_target_pairs={{0,2},{4,0},{8,4},{12,8},{14,12},{10,14},{6,10},{2,6},{1,3},{5,1},... | collective-permute-start | bytes 786440 | tf_op jit(solution)/shard_map/ppermute | solution.py:125
  36.0 2.5 %collective-permute-done.4 = bf16[256,512]{1,0:T(8,128)(2,1)S(1)} collective-permute-done((bf16[256,512]{1,0:T(8,128)(2,1)S(1)}, bf16[256,512]{1,0:T(8,128)(2,1)S(1)}, u32[]{:S(2)}, u32[]{:S(2)}) %collective-permute-start.4) | collective-permute-done | bytes 262176 | tf_op jit(solution)/shard_map/ppermute | solution.py:125
  38.5 1.8 %collective-permute-start.5 = (bf16[256,512]{1,0:T(8,128)(2,1)S(1)}, bf16[256,512]{1,0:T(8,128)(2,1)S(1)}, u32[]{:S(2)}, u32[]{:S(2)}) collective-permute-start(bf16[256,512]{1,0:T(8,128)(2,1)S(1)} %fusion.7), channel_id=1, source_target_pairs={{0,4},{4,8},{8,12},{12,14},{14,10},{10,6},{6,2},{2,0},{1,5},{5,9},... | collective-permute-start | bytes 786440 | tf_op jit(solution)/shard_map/ppermute | solution.py:125
  41.1 4.3 %shard_map.428 = (f32[5,256,512]{2,1,0:T(8,128)S(1)}, f32[5,256,512]{2,1,0:T(8,128)S(1)}) custom-call(s32[5]{0:T(128)S(1)} %get-tuple-element.245.spot, bf16[512,512]{1,0:T(8,128)(2,1)S(1)} %copy-done.3, bf16[512,512]{1,0:T(8,128)(2,1)S(1)} %collective-permute-done.far, bf16[512,8192]{1,0:T(8,128)(2,1)S(1)} %copy-done.2, ...), custom_call_target="tpu_custom_call" | custom-call | flops 2684354560 | bytes 5242880 | tf_op jit(solution)/shard_map/pallas_call | solution.py:168
  48.9 3.4 %collective-permute-done.15 = bf16[256,512]{1,0:T(8,128)(2,1)S(1)} collective-permute-done((bf16[256,512]{1,0:T(8,128)(2,1)S(1)}, bf16[256,512]{1,0:T(8,128)(2,1)S(1)}, u32[]{:S(2)}, u32[]{:S(2)}) %collective-permute-start.15) | collective-permute-done | bytes 262176 | tf_op jit(solution)/shard_map/ppermute | solution.py:125
  52.4 5.5 %collective-permute-done.9 = bf16[256,512]{1,0:T(8,128)(2,1)S(1)} collective-permute-done((bf16[256,512]{1,0:T(8,128)(2,1)S(1)}, bf16[256,512]{1,0:T(8,128)(2,1)S(1)}, u32[]{:S(2)}, u32[]{:S(2)}) %collective-permute-start.9) | collective-permute-done | bytes 262176 | tf_op jit(solution)/shard_map/ppermute | solution.py:125
  58.0 1.6 collective-permute-start.6
  59.7 2.8 %collective-permute-done.16 = bf16[256,512]{1,0:T(8,128)(2,1)S(1)} collective-permute-done((bf16[256,512]{1,0:T(8,128)(2,1)S(1)}, bf16[256,512]{1,0:T(8,128)(2,1)S(1)}, u32[]{:S(2)}, u32[]{:S(2)}) %collective-permute-start.16) | collective-permute-done | bytes 262176 | tf_op jit(solution)/shard_map/ppermute | solution.py:125
  62.6 1.6 collective-permute-start.12
  65.1 1.8 %collective-permute-start.7 = (bf16[256,512]{1,0:T(8,128)(2,1)S(1)}, bf16[256,512]{1,0:T(8,128)(2,1)S(1)}, u32[]{:S(2)}, u32[]{:S(2)}) collective-permute-start(bf16[256,512]{1,0:T(8,128)(2,1)S(1)} %fusion.9), channel_id=1, source_target_pairs={{0,4},{4,8},{8,12},{12,14},{14,10},{10,6},{6,2},{2,0},{1,5},{5,9},... | collective-permute-start | bytes 786440 | tf_op jit(solution)/shard_map/ppermute | solution.py:125
  66.8 5.0 %collective-permute-done.12 = bf16[256,512]{1,0:T(8,128)(2,1)S(1)} collective-permute-done((bf16[256,512]{1,0:T(8,128)(2,1)S(1)}, bf16[256,512]{1,0:T(8,128)(2,1)S(1)}, u32[]{:S(2)}, u32[]{:S(2)}) %collective-permute-start.12) | collective-permute-done | bytes 262176 | tf_op jit(solution)/shard_map/ppermute | solution.py:125
  71.9 1.6 collective-permute-start.13
  73.6 3.9 %collective-permute-done.7.first = bf16[256,512]{1,0:T(8,128)(2,1)S(1)} collective-permute-done((bf16[256,512]{1,0:T(8,128)(2,1)S(1)}, bf16[256,512]{1,0:T(8,128)(2,1)S(1)}, u32[]{:S(2)}, u32[]{:S(2)}) %collective-permute-start.7) | collective-permute-done | bytes 262176 | tf_op jit(solution)/shard_map/ppermute | solution.py:125
  78.4 2.9 %collective-permute-done.13.first = bf16[256,512]{1,0:T(8,128)(2,1)S(1)} collective-permute-done((bf16[256,512]{1,0:T(8,128)(2,1)S(1)}, bf16[256,512]{1,0:T(8,128)(2,1)S(1)}, u32[]{:S(2)}, u32[]{:S(2)}) %collective-permute-start.13) | collective-permute-done | bytes 262176 | tf_op jit(solution)/shard_map/ppermute | solution.py:125
  83.3 3.1 %collective-permute-done.19 = f32[2,256]{1,0:T(2,128)S(1)} collective-permute-done((f32[2,256]{1,0:T(2,128)S(1)}, f32[2,256]{1,0:T(2,128)S(1)}, u32[]{:S(2)}, u32[]{:S(2)}) %collective-permute-start.19) | collective-permute-done | bytes 2080 | tf_op jit(solution)/shard_map/ppermute | solution.py:134
  86.5 1.6 collective-permute-start.20
  88.1 2.0 %collective-permute-done.20 = f32[2,256]{1,0:T(2,128)S(1)} collective-permute-done((f32[2,256]{1,0:T(2,128)S(1)}, f32[2,256]{1,0:T(2,128)S(1)}, u32[]{:S(2)}, u32[]{:S(2)}) %collective-permute-start.20) | collective-permute-done | bytes 2080 | tf_op jit(solution)/shard_map/ppermute | solution.py:134
  90.1 2.6 %collective-permute-start.21 = (f32[2,256]{1,0:T(2,128)S(1)}, f32[2,256]{1,0:T(2,128)S(1)}, u32[]{:S(2)}, u32[]{:S(2)}) collective-permute-start(f32[2,256]{1,0:T(2,128)S(1)} %add.673), channel_id=1, source_target_pairs={{0,8},{2,10},{4,12},{6,14},{8,0},{10,2},{12,4},{14,6},{1,9},{3,11}... | collective-permute-start | bytes 6152 | tf_op jit(solution)/shard_map/ppermute | solution.py:134
  92.7 1.9 %collective-permute-done.21 = f32[2,256]{1,0:T(2,128)S(1)} collective-permute-done((f32[2,256]{1,0:T(2,128)S(1)}, f32[2,256]{1,0:T(2,128)S(1)}, u32[]{:S(2)}, u32[]{:S(2)}) %collective-permute-start.21) | collective-permute-done | bytes 2080 | tf_op jit(solution)/shard_map/ppermute | solution.py:134
  95.6 1.6 collective-permute-start.38
  97.5 1.6 collective-permute-start.22
  100.2 4.2 %collective-permute-done.27.refs_4_ = bf16[264,512]{1,0:T(8,128)(2,1)S(1)} collective-permute-done((bf16[264,512]{1,0:T(8,128)(2,1)S(1)}, bf16[264,512]{1,0:T(8,128)(2,1)S(1)}, u32[]{:S(2)}, u32[]{:S(2)}) %collective-permute-start.27) | collective-permute-done | bytes 270368 | tf_op jit(solution)/shard_map/ppermute | solution.py:125
  104.9 5.0 %collective-permute-done.22.refs_0_ = bf16[264,512]{1,0:T(8,128)(2,1)S(1)} collective-permute-done((bf16[264,512]{1,0:T(8,128)(2,1)S(1)}, bf16[264,512]{1,0:T(8,128)(2,1)S(1)}, u32[]{:S(2)}, u32[]{:S(2)}) %collective-permute-start.22) | collective-permute-done | bytes 270368 | tf_op jit(solution)/shard_map/ppermute | solution.py:125
  110.6 1.5 collective-permute-start.28
  112.6 1.6 collective-permute-start.23
  114.7 5.2 %collective-permute-done.28.refs_4_ = bf16[264,512]{1,0:T(8,128)(2,1)S(1)} collective-permute-done((bf16[264,512]{1,0:T(8,128)(2,1)S(1)}, bf16[264,512]{1,0:T(8,128)(2,1)S(1)}, u32[]{:S(2)}, u32[]{:S(2)}) %collective-permute-start.28) | collective-permute-done | bytes 270368 | tf_op jit(solution)/shard_map/ppermute | solution.py:125
  120.0 1.5 collective-permute-done.39.refs_6_
  121.5 5.0 %collective-permute-done.23.refs_0_ = bf16[264,512]{1,0:T(8,128)(2,1)S(1)} collective-permute-done((bf16[264,512]{1,0:T(8,128)(2,1)S(1)}, bf16[264,512]{1,0:T(8,128)(2,1)S(1)}, u32[]{:S(2)}, u32[]{:S(2)}) %collective-permute-start.23) | collective-permute-done | bytes 270368 | tf_op jit(solution)/shard_map/ppermute | solution.py:125
  127.2 1.6 collective-permute-start.29
  132.9 1.5 collective-permute-start.35
  135.1 1.6 collective-permute-done.29.refs_4_
  137.4 1.6 collective-permute-start.30
  140.3 4.7 %collective-permute-done.40.refs_6_ = bf16[264,512]{1,0:T(8,128)(2,1)} collective-permute-done((bf16[264,512]{1,0:T(8,128)(2,1)S(1)}, bf16[264,512]{1,0:T(8,128)(2,1)}, u32[]{:S(2)}, u32[]{:S(2)}) %collective-permute-start.40) | collective-permute-done | bytes 270368 | tf_op jit(solution)/shard_map/ppermute | solution.py:125
  151.8 1.9 %pad_maximum_fusion = bf16[512,512]{1,0:T(8,128)(2,1)} fusion(bf16[256,512]{1,0:T(8,128)(2,1)} %copy-done.26, bf16[256,512]{1,0:T(8,128)(2,1)} %copy-done.25), kind=kLoop, calls=%fused_computation.4 | loop fusion | flops 1048576 | bytes 1048576 | tf_op jit(solution)/shard_map/concatenate | solution.py:294
  155.6 1.6 shard_map.437
  158.1 2.0 %shard_map.438 = (bf16[512,8192]{1,0:T(8,128)(2,1)}, bf16[2,128,512]{2,1,0:T(8,128)(2,1)S(1)}) custom-call(s32[8]{0:T(128)S(1)} %concatenate.25.spot, bf16[264,512]{1,0:T(8,128)(2,1)S(1)} %collective-permute-done.22.refs_0_, bf16[264,512]{1,0:T(8,128)(2,1)S(1)} %collective-permute-done.46.refs_1_, ...), custom_call_target="tpu_custom_call", output_to_operand_aliasing={{0}: (9, {}), {1}: (10, {})} | custom-call | flops 100000000 | bytes 4194304 | tf_op jit(solution)/shard_map/pallas_call | solution.py:246
  160.2 2.0 %shard_map.439 = (bf16[512,8192]{1,0:T(8,128)(2,1)}, bf16[2,128,512]{2,1,0:T(8,128)(2,1)S(1)}) custom-call(s32[8]{0:T(128)S(1)} %concatenate.24.spot, bf16[264,512]{1,0:T(8,128)(2,1)S(1)} %copy-done.6, bf16[264,512]{1,0:T(8,128)(2,1)S(1)} %copy-done.16, bf16[264,512]{1,0:T(8,128)(2,1)S(1)} %copy-done.8, ...), custom_call_target="tpu_custom_call", output_to_operand_aliasing={{0}: (9, {}), {1}: (10, {})} | custom-call | flops 100000000 | bytes 4194304 | tf_op jit(solution)/shard_map/pallas_call | solution.py:246
  162.3 2.9 %shard_map.440 = (bf16[512,8192]{1,0:T(8,128)(2,1)}, bf16[2,128,512]{2,1,0:T(8,128)(2,1)S(1)}) custom-call(s32[8]{0:T(128)S(1)} %concatenate.23.spot, bf16[264,512]{1,0:T(8,128)(2,1)} %collective-permute-done.24.refs_0_, bf16[264,512]{1,0:T(8,128)(2,1)} %collective-permute-done.32.refs_1_, ...), custom_call_target="tpu_custom_call", output_to_operand_aliasing={{0}: (9, {}), {1}: (10, {})} | custom-call | flops 100000000 | bytes 4194304 | tf_op jit(solution)/shard_map/pallas_call | solution.py:246
  165.2 1.6 shard_map.441
  (167 shorter events, 31.2 us)
Async XLA Ops:
  10.4 30.7 %collective-permute-start.1 = (bf16[5,512,512]{2,1,0:T(8,128)(2,1)}, bf16[5,512,512]{2,1,0:T(8,128)(2,1)S(1)}, u32[]{:S(2)}, u32[]{:S(2)}) collective-permute-start(bf16[5,512,512]{2,1,0:T(8,128)(2,1)} %shard_map.427), channel_id=1, source_target_pairs={{0,1},{1,0},{2,3},{3,2},{4,5},{5,4},{6,7},{7,6},{8,9},{9,8},{10,11... | collective-permute-start | bytes 7864328 | tf_op jit(solution)/shard_map/ppermute | solution.py:128
  16.4 15.4 %collective-permute-start.2 = (bf16[2,512,512]{2,1,0:T(8,128)(2,1)S(1)}, bf16[2,512,512]{2,1,0:T(8,128)(2,1)S(1)}, u32[]{:S(2)}, u32[]{:S(2)}) collective-permute-start(bf16[2,512,512]{2,1,0:T(8,128)(2,1)S(1)} %shard_map.429), channel_id=1, source_target_pairs={{0,1},{1,0},{2,3},{3,2},{4,5},{5,4},{6,7},{7,6},{8,9},{9,8},{10,11... | collective-permute-start | bytes 3145736 | tf_op jit(solution)/shard_map/ppermute | solution.py:128
  16.7 9.9 %collective-permute-start = (bf16[512,512]{1,0:T(8,128)(2,1)S(1)}, bf16[512,512]{1,0:T(8,128)(2,1)S(1)}, u32[]{:S(2)}, u32[]{:S(2)}) collective-permute-start(bf16[512,512]{1,0:T(8,128)(2,1)S(1)} %copy-done.3), channel_id=1, source_target_pairs={{0,1},{1,0},{2,3},{3,2},{4,5},{5,4},{6,7},{7,6},{8,9},{9,8},{10,11... | collective-permute-start | bytes 1572872 | tf_op jit(solution)/shard_map/ppermute | solution.py:128
  28.9 9.5 %collective-permute-start.4 = (bf16[256,512]{1,0:T(8,128)(2,1)S(1)}, bf16[256,512]{1,0:T(8,128)(2,1)S(1)}, u32[]{:S(2)}, u32[]{:S(2)}) collective-permute-start(bf16[256,512]{1,0:T(8,128)(2,1)S(1)} %bitcast.71), channel_id=1, source_target_pairs={{0,4},{4,8},{8,12},{12,14},{14,10},{10,6},{6,2},{2,0},{1,5},{5,9},... | collective-permute-start | bytes 786440 | tf_op jit(solution)/shard_map/ppermute | solution.py:125
  31.8 9.2 %collective-permute-start.14 = (bf16[256,512]{1,0:T(8,128)(2,1)S(1)}, bf16[256,512]{1,0:T(8,128)(2,1)S(1)}, u32[]{:S(2)}, u32[]{:S(2)}) collective-permute-start(bf16[256,512]{1,0:T(8,128)(2,1)S(1)} %bitcast.70), channel_id=1, source_target_pairs={{0,2},{4,0},{8,4},{12,8},{14,12},{10,14},{6,10},{2,6},{1,3},{5,1},... | collective-permute-start | bytes 786440 | tf_op jit(solution)/shard_map/ppermute | solution.py:125
  34.0 12.7 %collective-permute-start.8 = (bf16[256,512]{1,0:T(8,128)(2,1)S(1)}, bf16[256,512]{1,0:T(8,128)(2,1)S(1)}, u32[]{:S(2)}, u32[]{:S(2)}) collective-permute-start(bf16[256,512]{1,0:T(8,128)(2,1)S(1)} %fusion.10), channel_id=1, source_target_pairs={{0,2},{4,0},{8,4},{12,8},{14,12},{10,14},{6,10},{2,6},{1,3},{5,1},... | collective-permute-start | bytes 786440 | tf_op jit(solution)/shard_map/ppermute | solution.py:125
  38.5 13.8 %collective-permute-start.5 = (bf16[256,512]{1,0:T(8,128)(2,1)S(1)}, bf16[256,512]{1,0:T(8,128)(2,1)S(1)}, u32[]{:S(2)}, u32[]{:S(2)}) collective-permute-start(bf16[256,512]{1,0:T(8,128)(2,1)S(1)} %fusion.7), channel_id=1, source_target_pairs={{0,4},{4,8},{8,12},{12,14},{14,10},{10,6},{6,2},{2,0},{1,5},{5,9},... | collective-permute-start | bytes 786440 | tf_op jit(solution)/shard_map/ppermute | solution.py:125
  41.1 11.2 %collective-permute-start.15 = (bf16[256,512]{1,0:T(8,128)(2,1)S(1)}, bf16[256,512]{1,0:T(8,128)(2,1)S(1)}, u32[]{:S(2)}, u32[]{:S(2)}) collective-permute-start(bf16[256,512]{1,0:T(8,128)(2,1)S(1)} %fusion), channel_id=1, source_target_pairs={{0,2},{4,0},{8,4},{12,8},{14,12},{10,14},{6,10},{2,6},{1,3},{5,1},... | collective-permute-start | bytes 786440 | tf_op jit(solution)/shard_map/ppermute | solution.py:125
  46.7 11.2 %collective-permute-start.9 = (bf16[256,512]{1,0:T(8,128)(2,1)S(1)}, bf16[256,512]{1,0:T(8,128)(2,1)S(1)}, u32[]{:S(2)}, u32[]{:S(2)}) collective-permute-start(bf16[256,512]{1,0:T(8,128)(2,1)S(1)} %fusion.5), channel_id=1, source_target_pairs={{0,2},{4,0},{8,4},{12,8},{14,12},{10,14},{6,10},{2,6},{1,3},{5,1},... | collective-permute-start | bytes 786440 | tf_op jit(solution)/shard_map/ppermute | solution.py:125
  47.6 12.0 %collective-permute-start.11 = (bf16[256,512]{1,0:T(8,128)(2,1)S(1)}, bf16[256,512]{1,0:T(8,128)(2,1)S(1)}, u32[]{:S(2)}, u32[]{:S(2)}) collective-permute-start(bf16[256,512]{1,0:T(8,128)(2,1)S(1)} %fusion.11), channel_id=1, source_target_pairs={{0,4},{4,8},{8,12},{12,14},{14,10},{10,6},{6,2},{2,0},{1,5},{5,9},... | collective-permute-start | bytes 786440 | tf_op jit(solution)/shard_map/ppermute | solution.py:125
  52.3 10.1 %collective-permute-start.16 = (bf16[256,512]{1,0:T(8,128)(2,1)S(1)}, bf16[256,512]{1,0:T(8,128)(2,1)S(1)}, u32[]{:S(2)}, u32[]{:S(2)}) collective-permute-start(bf16[256,512]{1,0:T(8,128)(2,1)S(1)} %fusion.1), channel_id=1, source_target_pairs={{0,2},{4,0},{8,4},{12,8},{14,12},{10,14},{6,10},{2,6},{1,3},{5,1},... | collective-permute-start | bytes 786440 | tf_op jit(solution)/shard_map/ppermute | solution.py:125
  58.0 7.0 %collective-permute-start.6 = (bf16[256,512]{1,0:T(8,128)(2,1)S(1)}, bf16[256,512]{1,0:T(8,128)(2,1)S(1)}, u32[]{:S(2)}, u32[]{:S(2)}) collective-permute-start(bf16[256,512]{1,0:T(8,128)(2,1)S(1)} %get-tuple-element.228), channel_id=1, source_target_pairs={{0,4},{4,8},{8,12},{12,14},{14,10},{10,6},{6,2},{2,0},{1,5},{5,9},... | collective-permute-start | bytes 786440 | tf_op jit(solution)/shard_map/ppermute | solution.py:125
  62.6 9.2 %collective-permute-start.12 = (bf16[256,512]{1,0:T(8,128)(2,1)S(1)}, bf16[256,512]{1,0:T(8,128)(2,1)S(1)}, u32[]{:S(2)}, u32[]{:S(2)}) collective-permute-start(bf16[256,512]{1,0:T(8,128)(2,1)S(1)} %get-tuple-element.230), channel_id=1, source_target_pairs={{0,4},{4,8},{8,12},{12,14},{14,10},{10,6},{6,2},{2,0},{1,5},{5,9},... | collective-permute-start | bytes 786440 | tf_op jit(solution)/shard_map/ppermute | solution.py:125
  64.2 9.3 %collective-permute-start.10 = (bf16[256,512]{1,0:T(8,128)(2,1)S(1)}, bf16[256,512]{1,0:T(8,128)(2,1)S(1)}, u32[]{:S(2)}, u32[]{:S(2)}) collective-permute-start(bf16[256,512]{1,0:T(8,128)(2,1)S(1)} %get-tuple-element.227), channel_id=1, source_target_pairs={{0,2},{4,0},{8,4},{12,8},{14,12},{10,14},{6,10},{2,6},{1,3},{5,1},... | collective-permute-start | bytes 786440 | tf_op jit(solution)/shard_map/ppermute | solution.py:125
  64.7 13.7 %collective-permute-start.17 = (bf16[256,512]{1,0:T(8,128)(2,1)S(1)}, bf16[256,512]{1,0:T(8,128)(2,1)S(1)}, u32[]{:S(2)}, u32[]{:S(2)}) collective-permute-start(bf16[256,512]{1,0:T(8,128)(2,1)S(1)} %get-tuple-element.229), channel_id=1, source_target_pairs={{0,2},{4,0},{8,4},{12,8},{14,12},{10,14},{6,10},{2,6},{1,3},{5,1},... | collective-permute-start | bytes 786440 | tf_op jit(solution)/shard_map/ppermute | solution.py:125
  65.1 12.4 %collective-permute-start.7 = (bf16[256,512]{1,0:T(8,128)(2,1)S(1)}, bf16[256,512]{1,0:T(8,128)(2,1)S(1)}, u32[]{:S(2)}, u32[]{:S(2)}) collective-permute-start(bf16[256,512]{1,0:T(8,128)(2,1)S(1)} %fusion.9), channel_id=1, source_target_pairs={{0,4},{4,8},{8,12},{12,14},{14,10},{10,6},{6,2},{2,0},{1,5},{5,9},... | collective-permute-start | bytes 786440 | tf_op jit(solution)/shard_map/ppermute | solution.py:125
  71.9 9.4 %collective-permute-start.13 = (bf16[256,512]{1,0:T(8,128)(2,1)S(1)}, bf16[256,512]{1,0:T(8,128)(2,1)S(1)}, u32[]{:S(2)}, u32[]{:S(2)}) collective-permute-start(bf16[256,512]{1,0:T(8,128)(2,1)S(1)} %fusion.4), channel_id=1, source_target_pairs={{0,4},{4,8},{8,12},{12,14},{14,10},{10,6},{6,2},{2,0},{1,5},{5,9},... | collective-permute-start | bytes 786440 | tf_op jit(solution)/shard_map/ppermute | solution.py:125
  90.1 4.5 %collective-permute-start.21 = (f32[2,256]{1,0:T(2,128)S(1)}, f32[2,256]{1,0:T(2,128)S(1)}, u32[]{:S(2)}, u32[]{:S(2)}) collective-permute-start(f32[2,256]{1,0:T(2,128)S(1)} %add.673), channel_id=1, source_target_pairs={{0,8},{2,10},{4,12},{6,14},{8,0},{10,2},{12,4},{14,6},{1,9},{3,11}... | collective-permute-start | bytes 6152 | tf_op jit(solution)/shard_map/ppermute | solution.py:134
  95.0 4.1 %collective-permute-start.51 = (bf16[264,512]{1,0:T(8,128)(2,1)S(1)}, bf16[264,512]{1,0:T(8,128)(2,1)S(1)}, u32[]{:S(2)}, u32[]{:S(2)}) collective-permute-start(bf16[264,512]{1,0:T(8,128)(2,1)S(1)} %shard_map.436.refs_2_), channel_id=1, source_target_pairs={{0,1},{1,0},{2,3},{3,2},{4,5},{5,4},{6,7},{7,6},{8,9},{9,8},{10,11... | collective-permute-start | bytes 811016 | tf_op jit(solution)/shard_map/ppermute | solution.py:128
  95.0 9.4 %collective-permute-start.27 = (bf16[264,512]{1,0:T(8,128)(2,1)S(1)}, bf16[264,512]{1,0:T(8,128)(2,1)S(1)}, u32[]{:S(2)}, u32[]{:S(2)}) collective-permute-start(bf16[264,512]{1,0:T(8,128)(2,1)S(1)} %shard_map.436.refs_2_), channel_id=1, source_target_pairs={{0,2},{4,0},{8,4},{12,8},{14,12},{10,14},{6,10},{2,6},{1,3},{5,1},... | collective-permute-start | bytes 811016 | tf_op jit(solution)/shard_map/ppermute | solution.py:125
  95.6 9.4 %collective-permute-start.38 = (bf16[264,512]{1,0:T(8,128)(2,1)S(1)}, bf16[264,512]{1,0:T(8,128)(2,1)S(1)}, u32[]{:S(2)}, u32[]{:S(2)}) collective-permute-start(bf16[264,512]{1,0:T(8,128)(2,1)S(1)} %shard_map.436.refs_2_), channel_id=1, source_target_pairs={{0,4},{4,8},{8,12},{12,14},{14,10},{10,6},{6,2},{2,0},{1,5},{5,9},... | collective-permute-start | bytes 811016 | tf_op jit(solution)/shard_map/ppermute | solution.py:125
  97.5 12.4 %collective-permute-start.22 = (bf16[264,512]{1,0:T(8,128)(2,1)S(1)}, bf16[264,512]{1,0:T(8,128)(2,1)S(1)}, u32[]{:S(2)}, u32[]{:S(2)}) collective-permute-start(bf16[264,512]{1,0:T(8,128)(2,1)S(1)} %shard_map.435.refs_0_), channel_id=1, source_target_pairs={{0,4},{4,8},{8,12},{12,14},{14,10},{10,6},{6,2},{2,0},{1,5},{5,9},... | collective-permute-start | bytes 811016 | tf_op jit(solution)/shard_map/ppermute | solution.py:125
  99.1 10.8 %collective-permute-start.50 = (bf16[264,512]{1,0:T(8,128)(2,1)S(1)}, bf16[264,512]{1,0:T(8,128)(2,1)S(1)}, u32[]{:S(2)}, u32[]{:S(2)}) collective-permute-start(bf16[264,512]{1,0:T(8,128)(2,1)S(1)} %shard_map.435.refs_0_), channel_id=1, source_target_pairs={{0,1},{1,0},{2,3},{3,2},{4,5},{5,4},{6,7},{7,6},{8,9},{9,8},{10,11... | collective-permute-start | bytes 811016 | tf_op jit(solution)/shard_map/ppermute | solution.py:128
  99.8 12.3 %collective-permute-start.33 = (bf16[264,512]{1,0:T(8,128)(2,1)S(1)}, bf16[264,512]{1,0:T(8,128)(2,1)S(1)}, u32[]{:S(2)}, u32[]{:S(2)}) collective-permute-start(bf16[264,512]{1,0:T(8,128)(2,1)S(1)} %shard_map.435.refs_0_), channel_id=1, source_target_pairs={{0,2},{4,0},{8,4},{12,8},{14,12},{10,14},{6,10},{2,6},{1,3},{5,1},... | collective-permute-start | bytes 811016 | tf_op jit(solution)/shard_map/ppermute | solution.py:125
  104.4 8.2 %collective-permute-start.48 = (bf16[264,512]{1,0:T(8,128)(2,1)S(1)}, bf16[264,512]{1,0:T(8,128)(2,1)S(1)}, u32[]{:S(2)}, u32[]{:S(2)}) collective-permute-start(bf16[264,512]{1,0:T(8,128)(2,1)S(1)} %collective-permute-done.27.refs_4_), channel_id=1, source_target_pairs={{0,1},{1,0},{2,3},{3,2},{4,5},{5,4},{6,7},{7,6},{8,9},{9,8},{10,11... | collective-permute-start | bytes 811016 | tf_op jit(solution)/shard_map/ppermute | solution.py:128
  104.9 9.3 %collective-permute-start.49 = (bf16[264,512]{1,0:T(8,128)(2,1)S(1)}, bf16[264,512]{1,0:T(8,128)(2,1)S(1)}, u32[]{:S(2)}, u32[]{:S(2)}) collective-permute-start(bf16[264,512]{1,0:T(8,128)(2,1)S(1)} %collective-permute-done.38.refs_6_), channel_id=1, source_target_pairs={{0,1},{1,0},{2,3},{3,2},{4,5},{5,4},{6,7},{7,6},{8,9},{9,8},{10,11... | collective-permute-start | bytes 811016 | tf_op jit(solution)/shard_map/ppermute | solution.py:128
  109.9 4.3 %collective-permute-start.46 = (bf16[264,512]{1,0:T(8,128)(2,1)S(1)}, bf16[264,512]{1,0:T(8,128)(2,1)S(1)}, u32[]{:S(2)}, u32[]{:S(2)}) collective-permute-start(bf16[264,512]{1,0:T(8,128)(2,1)S(1)} %collective-permute-done.22.refs_0_), channel_id=1, source_target_pairs={{0,1},{1,0},{2,3},{3,2},{4,5},{5,4},{6,7},{7,6},{8,9},{9,8},{10,11... | collective-permute-start | bytes 811016 | tf_op jit(solution)/shard_map/ppermute | solution.py:128
  110.6 9.4 %collective-permute-start.28 = (bf16[264,512]{1,0:T(8,128)(2,1)S(1)}, bf16[264,512]{1,0:T(8,128)(2,1)S(1)}, u32[]{:S(2)}, u32[]{:S(2)}) collective-permute-start(bf16[264,512]{1,0:T(8,128)(2,1)S(1)} %collective-permute-done.27.refs_4_), channel_id=1, source_target_pairs={{0,2},{4,0},{8,4},{12,8},{14,12},{10,14},{6,10},{2,6},{1,3},{5,1},... | collective-permute-start | bytes 811016 | tf_op jit(solution)/shard_map/ppermute | solution.py:125
  112.1 9.4 %collective-permute-start.39 = (bf16[264,512]{1,0:T(8,128)(2,1)S(1)}, bf16[264,512]{1,0:T(8,128)(2,1)S(1)}, u32[]{:S(2)}, u32[]{:S(2)}) collective-permute-start(bf16[264,512]{1,0:T(8,128)(2,1)S(1)} %collective-permute-done.38.refs_6_), channel_id=1, source_target_pairs={{0,4},{4,8},{8,12},{12,14},{14,10},{10,6},{6,2},{2,0},{1,5},{5,9},... | collective-permute-start | bytes 811016 | tf_op jit(solution)/shard_map/ppermute | solution.py:125
  112.6 13.9 %collective-permute-start.23 = (bf16[264,512]{1,0:T(8,128)(2,1)S(1)}, bf16[264,512]{1,0:T(8,128)(2,1)S(1)}, u32[]{:S(2)}, u32[]{:S(2)}) collective-permute-start(bf16[264,512]{1,0:T(8,128)(2,1)S(1)} %collective-permute-done.22.refs_0_), channel_id=1, source_target_pairs={{0,4},{4,8},{8,12},{12,14},{14,10},{10,6},{6,2},{2,0},{1,5},{5,9},... | collective-permute-start | bytes 811016 | tf_op jit(solution)/shard_map/ppermute | solution.py:125
  114.2 12.3 %collective-permute-start.47 = (bf16[264,512]{1,0:T(8,128)(2,1)S(1)}, bf16[264,512]{1,0:T(8,128)(2,1)S(1)}, u32[]{:S(2)}, u32[]{:S(2)}) collective-permute-start(bf16[264,512]{1,0:T(8,128)(2,1)S(1)} %collective-permute-done.33.refs_2_), channel_id=1, source_target_pairs={{0,1},{1,0},{2,3},{3,2},{4,5},{5,4},{6,7},{7,6},{8,9},{9,8},{10,11... | collective-permute-start | bytes 811016 | tf_op jit(solution)/shard_map/ppermute | solution.py:128
  114.2 14.6 %collective-permute-start.34 = (bf16[264,512]{1,0:T(8,128)(2,1)S(1)}, bf16[264,512]{1,0:T(8,128)(2,1)S(1)}, u32[]{:S(2)}, u32[]{:S(2)}) collective-permute-start(bf16[264,512]{1,0:T(8,128)(2,1)S(1)} %collective-permute-done.33.refs_2_), channel_id=1, source_target_pairs={{0,2},{4,0},{8,4},{12,8},{14,12},{10,14},{6,10},{2,6},{1,3},{5,1},... | collective-permute-start | bytes 811016 | tf_op jit(solution)/shard_map/ppermute | solution.py:125
  120.0 9.1 %collective-permute-start.44 = (bf16[264,512]{1,0:T(8,128)(2,1)S(1)}, bf16[264,512]{1,0:T(8,128)(2,1)S(1)}, u32[]{:S(2)}, u32[]{:S(2)}) collective-permute-start(bf16[264,512]{1,0:T(8,128)(2,1)S(1)} %collective-permute-done.28.refs_4_), channel_id=1, source_target_pairs={{0,1},{1,0},{2,3},{3,2},{4,5},{5,4},{6,7},{7,6},{8,9},{9,8},{10,11... | collective-permute-start | bytes 811016 | tf_op jit(solution)/shard_map/ppermute | solution.py:128
  121.5 9.5 %collective-permute-start.45 = (bf16[264,512]{1,0:T(8,128)(2,1)S(1)}, bf16[264,512]{1,0:T(8,128)(2,1)S(1)}, u32[]{:S(2)}, u32[]{:S(2)}) collective-permute-start(bf16[264,512]{1,0:T(8,128)(2,1)S(1)} %collective-permute-done.39.refs_6_), channel_id=1, source_target_pairs={{0,1},{1,0},{2,3},{3,2},{4,5},{5,4},{6,7},{7,6},{8,9},{9,8},{10,11... | collective-permute-start | bytes 811016 | tf_op jit(solution)/shard_map/ppermute | solution.py:128
  126.5 5.7 %collective-permute-start.42 = (bf16[264,512]{1,0:T(8,128)(2,1)S(1)}, bf16[264,512]{1,0:T(8,128)(2,1)S(1)}, u32[]{:S(2)}, u32[]{:S(2)}) collective-permute-start(bf16[264,512]{1,0:T(8,128)(2,1)S(1)} %collective-permute-done.23.refs_0_), channel_id=1, source_target_pairs={{0,1},{1,0},{2,3},{3,2},{4,5},{5,4},{6,7},{7,6},{8,9},{9,8},{10,11... | collective-permute-start | bytes 811016 | tf_op jit(solution)/shard_map/ppermute | solution.py:128
  127.2 9.5 %collective-permute-start.29 = (bf16[264,512]{1,0:T(8,128)(2,1)S(1)}, bf16[264,512]{1,0:T(8,128)(2,1)}, u32[]{:S(2)}, u32[]{:S(2)}) collective-permute-start(bf16[264,512]{1,0:T(8,128)(2,1)S(1)} %collective-permute-done.28.refs_4_), channel_id=1, source_target_pairs={{0,2},{4,0},{8,4},{12,8},{14,12},{10,14},{6,10},{2,6},{1,3},{5,1},... | collective-permute-start | bytes 811016 | tf_op jit(solution)/shard_map/ppermute | solution.py:125
  128.8 7.9 %collective-permute-start.43 = (bf16[264,512]{1,0:T(8,128)(2,1)S(1)}, bf16[264,512]{1,0:T(8,128)(2,1)S(1)}, u32[]{:S(2)}, u32[]{:S(2)}) collective-permute-start(bf16[264,512]{1,0:T(8,128)(2,1)S(1)} %collective-permute-done.34.refs_2_), channel_id=1, source_target_pairs={{0,1},{1,0},{2,3},{3,2},{4,5},{5,4},{6,7},{7,6},{8,9},{9,8},{10,11... | collective-permute-start | bytes 811016 | tf_op jit(solution)/shard_map/ppermute | solution.py:128
  129.8 9.5 %collective-permute-start.24 = (bf16[264,512]{1,0:T(8,128)(2,1)S(1)}, bf16[264,512]{1,0:T(8,128)(2,1)}, u32[]{:S(2)}, u32[]{:S(2)}) collective-permute-start(bf16[264,512]{1,0:T(8,128)(2,1)S(1)} %collective-permute-done.23.refs_0_), channel_id=1, source_target_pairs={{0,4},{4,8},{8,12},{12,14},{14,10},{10,6},{6,2},{2,0},{1,5},{5,9},... | collective-permute-start | bytes 811016 | tf_op jit(solution)/shard_map/ppermute | solution.py:125
  131.6 13.4 %collective-permute-start.40 = (bf16[264,512]{1,0:T(8,128)(2,1)S(1)}, bf16[264,512]{1,0:T(8,128)(2,1)}, u32[]{:S(2)}, u32[]{:S(2)}) collective-permute-start(bf16[264,512]{1,0:T(8,128)(2,1)S(1)} %collective-permute-done.39.refs_6_), channel_id=1, source_target_pairs={{0,4},{4,8},{8,12},{12,14},{14,10},{10,6},{6,2},{2,0},{1,5},{5,9},... | collective-permute-start | bytes 811016 | tf_op jit(solution)/shard_map/ppermute | solution.py:125
  132.9 12.1 %collective-permute-start.35 = (bf16[264,512]{1,0:T(8,128)(2,1)S(1)}, bf16[264,512]{1,0:T(8,128)(2,1)}, u32[]{:S(2)}, u32[]{:S(2)}) collective-permute-start(bf16[264,512]{1,0:T(8,128)(2,1)S(1)} %collective-permute-done.34.refs_2_), channel_id=1, source_target_pairs={{0,2},{4,0},{8,4},{12,8},{14,12},{10,14},{6,10},{2,6},{1,3},{5,1},... | collective-permute-start | bytes 811016 | tf_op jit(solution)/shard_map/ppermute | solution.py:125
  136.7 8.8 %collective-permute-start.37 = (bf16[264,512]{1,0:T(8,128)(2,1)}, bf16[264,512]{1,0:T(8,128)(2,1)S(1)}, u32[]{:S(2)}, u32[]{:S(2)}) collective-permute-start(bf16[264,512]{1,0:T(8,128)(2,1)} %collective-permute-done.29.refs_4_), channel_id=1, source_target_pairs={{0,1},{1,0},{2,3},{3,2},{4,5},{5,4},{6,7},{7,6},{8,9},{9,8},{10,11... | collective-permute-start | bytes 811016 | tf_op jit(solution)/shard_map/ppermute | solution.py:128
  137.4 13.6 %collective-permute-start.30 = (bf16[264,512]{1,0:T(8,128)(2,1)}, bf16[264,512]{1,0:T(8,128)(2,1)S(1)}, u32[]{:S(2)}, u32[]{:S(2)}) collective-permute-start(bf16[264,512]{1,0:T(8,128)(2,1)} %collective-permute-done.29.refs_4_), channel_id=1, source_target_pairs={{0,2},{4,0},{8,4},{12,8},{14,12},{10,14},{6,10},{2,6},{1,3},{5,1},... | collective-permute-start | bytes 811016 | tf_op jit(solution)/shard_map/ppermute | solution.py:125
  139.2 12.4 %collective-permute-start.25 = (bf16[264,512]{1,0:T(8,128)(2,1)}, bf16[264,512]{1,0:T(8,128)(2,1)S(1)}, u32[]{:S(2)}, u32[]{:S(2)}) collective-permute-start(bf16[264,512]{1,0:T(8,128)(2,1)} %collective-permute-done.24.refs_0_), channel_id=1, source_target_pairs={{0,4},{4,8},{8,12},{12,14},{14,10},{10,6},{6,2},{2,0},{1,5},{5,9},... | collective-permute-start | bytes 811016 | tf_op jit(solution)/shard_map/ppermute | solution.py:125
  145.0 17.2 %collective-permute-start.32 = (bf16[264,512]{1,0:T(8,128)(2,1)}, bf16[264,512]{1,0:T(8,128)(2,1)}, u32[]{:S(2)}, u32[]{:S(2)}) collective-permute-start(bf16[264,512]{1,0:T(8,128)(2,1)} %collective-permute-done.24.refs_0_), channel_id=1, source_target_pairs={{0,1},{1,0},{2,3},{3,2},{4,5},{5,4},{6,7},{7,6},{8,9},{9,8},{10,11... | collective-permute-start | bytes 811016 | tf_op jit(solution)/shard_map/ppermute | solution.py:128
  145.0 17.2 %collective-permute-start.41 = (bf16[264,512]{1,0:T(8,128)(2,1)}, bf16[264,512]{1,0:T(8,128)(2,1)}, u32[]{:S(2)}, u32[]{:S(2)}) collective-permute-start(bf16[264,512]{1,0:T(8,128)(2,1)} %collective-permute-done.40.refs_6_), channel_id=1, source_target_pairs={{0,1},{1,0},{2,3},{3,2},{4,5},{5,4},{6,7},{7,6},{8,9},{9,8},{10,11... | collective-permute-start | bytes 811016 | tf_op jit(solution)/shard_map/ppermute | solution.py:128
  146.2 16.0 %collective-permute-start.36 = (bf16[264,512]{1,0:T(8,128)(2,1)}, bf16[264,512]{1,0:T(8,128)(2,1)}, u32[]{:S(2)}, u32[]{:S(2)}) collective-permute-start(bf16[264,512]{1,0:T(8,128)(2,1)} %collective-permute-done.35.refs_2_), channel_id=1, source_target_pairs={{0,1},{1,0},{2,3},{3,2},{4,5},{5,4},{6,7},{7,6},{8,9},{9,8},{10,11... | collective-permute-start | bytes 811016 | tf_op jit(solution)/shard_map/ppermute | solution.py:128
  151.1 14.1 %collective-permute-start.31 = (bf16[264,512]{1,0:T(8,128)(2,1)S(1)}, bf16[264,512]{1,0:T(8,128)(2,1)S(1)}, u32[]{:S(2)}, u32[]{:S(2)}) collective-permute-start(bf16[264,512]{1,0:T(8,128)(2,1)S(1)} %collective-permute-done.30.refs_2_), channel_id=1, source_target_pairs={{0,1},{1,0},{2,3},{3,2},{4,5},{5,4},{6,7},{7,6},{8,9},{9,8},{10,11... | collective-permute-start | bytes 811016 | tf_op jit(solution)/shard_map/ppermute | solution.py:128
  151.6 13.6 %collective-permute-start.26 = (bf16[264,512]{1,0:T(8,128)(2,1)S(1)}, bf16[264,512]{1,0:T(8,128)(2,1)S(1)}, u32[]{:S(2)}, u32[]{:S(2)}) collective-permute-start(bf16[264,512]{1,0:T(8,128)(2,1)S(1)} %collective-permute-done.25.refs_0_), channel_id=1, source_target_pairs={{0,1},{1,0},{2,3},{3,2},{4,5},{5,4},{6,7},{7,6},{8,9},{9,8},{10,11... | collective-permute-start | bytes 811016 | tf_op jit(solution)/shard_map/ppermute | solution.py:128
  (34 other events, 158.5 us)
